TPU v7x, 32 devices: a whole 2x2x4 slice. The times are simulated.
32 devices in a mesh: row: 4 (over y, x), col: 8 (over z, core).
Axes of the slice: x: 2, y: 2, z: 4, core: 2. Of those that a mesh axis runs over, the one named last changes fastest.
Arguments:
- pair_states: bfloat16 [1024, 16384], P(None, ('row', 'col')), may hold values from -0.046875 to 0.046875
- screening: bfloat16 [4, 16384, 16384], P(None, 'row', 'col'), may hold values from -6 to 6
- qp_energy: float32 [8], replicated, may hold values from -0.5 to 0.5
- band_energy: float32 [2048], replicated, may hold values from -2 to 2
- band_index: int32 [128], replicated, may hold values from 0 to 2047
- nodes: float32 [4], replicated, may hold values from 0.1 to 2
- node_weights: float32 [4], replicated, may hold values from 0.05 to 1
Outputs:
- contrib: float32 [8, 128], replicated
- sigma: float32 [8], replicated
All inputs are finite; a program needn't handle non-finite values.
Results may differ from a plain program's by a relative error of at most 0.0003.
Values may be sent and summed in bfloat16 or wider, within the bound.
A program may use at most 128 MiB of HBM per device.

v0:
```python
import jax
import jax.numpy as jnp
from jax import lax
from jax.sharding import PartitionSpec as P


def broadcast(block, axis, holder):
    block = jnp.where(lax.axis_index(axis) == holder, block, jnp.zeros_like(block))
    return lax.psum(block, axis)


def shards(pair_states, screening, qp_energy, band_energy, band_index, nodes, node_weights):
    width = screening.shape[2]
    panel = lax.all_gather(pair_states, "col", axis=1, tiled=True)
    images = jnp.einsum("pg,fgc->fpc", panel, screening, preferred_element_type=jnp.float32)
    ratio = lax.axis_size("col") // lax.axis_size("row")
    column = lax.axis_index("col")
    offset = column % ratio * width
    own_piece = lax.dynamic_slice_in_dim(panel, offset, width, 1)
    col_states = broadcast(own_piece, "row", column // ratio)
    partial_value = jnp.sum(images * col_states.astype(jnp.float32)[None, :, :], axis=2)
    table = lax.broadcasted_iota(jnp.int32, (band_index.shape[0], band_energy.shape[0]), 1)
    chosen = jnp.sum(
        jnp.where(band_index[:, None] == table, band_energy[None, :], jnp.float32(0.0)), axis=1
    )
    gap = (qp_energy[:, None] - chosen[None, :]).reshape(-1)
    factor = (
        node_weights[:, None]
        * gap[None, :]
        / (gap[None, :] * gap[None, :] + nodes[:, None] * nodes[:, None])
    )
    flat = lax.psum(jnp.sum(factor * partial_value, axis=0), ("row", "col"))
    contrib = flat.reshape(qp_energy.shape[0], band_index.shape[0])
    sigma = jnp.sum(contrib, axis=1)
    return (contrib, sigma)


def solution(mesh):
    in_specs = (P(None, ("row", "col")), P(None, "row", "col"), P(), P(), P(), P(), P())
    out_specs = (P(), P())
    return jax.shard_map(shards, mesh=mesh, in_specs=in_specs, out_specs=out_specs, check_vma=False)
```

profile of v0, /device:TPU:0, one launch (start us, length us, event | category | flops | bytes accessed | tf_op | source)
XLA Modules:
  0.0 333.2 jit_solution(11457879454940917840)
XLA Ops:
  7.2 0.0 copy-start.8
  7.2 0.0 copy-start.3
  7.2 0.0 copy-start.5
  7.2 0.0 copy-start.4
  7.2 0.0 all-gather.2.cloned.1.call-start
  7.2 0.7 all-gather.2.cloned.1.call-update
  7.9 0.0 all-reduce.2.cloned.1.call-start
  8.0 86.4 %all-gather.2.cloned.1.call-done = bf16[1024,4096]{1,0:T(8,128)(2,1)} async-done(((bf16[1024,512]{1,0:T(8,128)(2,1)}), bf16[1024,4096]{1,0:T(8,128)(2,1)}) %all-gather.2.cloned.1.call-update) | async-done | bytes 8388624 | tf_op jit(solution)/shard_map/all_gather | solution.py:14
  94.4 5.5 %dynamic-slice_select_fusion = bf16[1024,2048]{1,0:T(8,128)(2,1)} fusion(bf16[1024,4096]{1,0:T(8,128)(2,1)} %all-gather.2.cloned.1.call-done, s32[]{:T(128)S(6)} %select_n.30, pred[]{:T(512)S(6)} %eq.15), kind=kLoop, calls=%fused_computation.3 | loop fusion | flops 2097152 | bytes 8388613 | tf_op jit(solution)/shard_map/jit(_where)/select_n | solution.py:8
  99.9 0.0 all-reduce.2.cloned.1.call-update
  99.9 0.0 copy-done.8
  99.9 0.5 mul.43
  100.4 0.0 copy-done.3
  100.4 0.0 copy-done.5
  100.4 0.2 select_reduce_fusion
  100.7 0.0 copy-done.4
  100.7 0.7 fusion.2
  101.4 0.7 subtract_bitcast_fusion
  102.0 100.2 %all-reduce.2.cloned.1.call-done = bf16[1024,2048]{1,0:T(8,128)(2,1)} async-done(((bf16[1024,2048]{1,0:T(8,128)(2,1)}), bf16[1024,2048]{1,0:T(8,128)(2,1)}) %all-reduce.2.cloned.1.call-update) | async-done | bytes 4194320 | tf_op jit(solution)/shard_map/psum | solution.py:9
  202.2 6.9 %copy.12 = f32[1024,2048]{0,1:T(8,128)} copy(bf16[1024,2048]{1,0:T(8,128)(2,1)} %all-reduce.2.cloned.1.call-done) | data formatting | bytes 12582912 | tf_op jit(solution)/shard_map/convert_element_type | solution.py:21
  209.0 0.0 copy-start.1
  209.0 0.0 copy-start.2
  209.0 0.0 copy-start.6
  209.0 0.0 copy-start.7
  209.1 77.2 %fusion = f32[4,1024]{1,0:T(4,128)S(1)} fusion(bf16[4,4096,2048]{2,1,0:T(8,128)(2,1)} %param.8, f32[1024,2048]{0,1:T(8,128)} %copy.12, bf16[1024,4096]{1,0:T(8,128)(2,1)} %all-gather.2.cloned.1.call-done), kind=kOutput, calls=%fused_computation.1 | convolution fusion | flops 68736253952 | bytes 83902464 | tf_op jit(solution)/shard_map/pg,fgc->fpc/dot_general | solution.py:15
  286.3 0.0 copy-done.1
  286.3 0.0 copy-done.2
  286.3 0.0 copy-done.6
  286.3 0.0 copy-done.7
  286.3 0.1 multiply_reduce_fusion
  286.4 39.3 %psum.15 = f32[8,128]{1,0:T(8,128)S(1)} all-reduce(f32[8,128]{1,0:T(8,128)S(1)} %bitcast.13), channel_id=1, replica_groups=mesh['row'=4,'col'=8] {'row','col'}, use_global_device_ids=true, to_apply=%region_4.5 | all-reduce | flops 1024 | bytes 8192 | tf_op jit(solution)/shard_map/psum | solution.py:32
  325.8 0.0 copy-start
  325.8 0.6 reduce_sum.39
  326.4 0.0 copy-done
Async XLA Ops:
  7.2 92.8 %copy-start.8 = (f32[4]{0:T(128)S(1)}, f32[4]{0:T(128)}, u32[]{:S(2)}) copy-start(f32[4]{0:T(128)} %param.12) | copy-start | bytes 52
  7.2 93.3 %copy-start.3 = (f32[2048]{0:T(1024)S(1)}, f32[2048]{0:T(1024)}, u32[]{:S(2)}) copy-start(f32[2048]{0:T(1024)} %param.10) | copy-start | bytes 24580
  7.2 93.3 %copy-start.5 = (s32[128]{0:T(128)S(1)}, s32[128]{0:T(128)}, u32[]{:S(2)}) copy-start(s32[128]{0:T(128)} %param.11) | copy-start | bytes 1540
  7.2 93.5 %copy-start.4 = (f32[8]{0:T(128)S(1)}, f32[8]{0:T(128)}, u32[]{:S(2)}) copy-start(f32[8]{0:T(128)} %param.9) | copy-start | bytes 100
  7.2 87.2 %all-gather.2.cloned.1.call-start = ((), (), s32[]{:S(2)}) async-start(), calls=%async_computation | async-start | bytes 9437184 | tf_op jit(solution)/shard_map/all_gather | solution.py:14
  7.9 194.2 %all-reduce.2.cloned.1.call-start = ((), (), s32[]{:S(2)}) async-start(), calls=%async_computation.1 | async-start | bytes 8388608 | tf_op jit(solution)/shard_map/psum | solution.py:9
  209.0 77.3 %copy-start.1 = (f32[1024]{0:T(1024)S(1)}, f32[1024]{0:T(1024)}, u32[]{:S(2)}) copy-start(f32[1024]{0:T(1024)} %fusion.2) | copy-start | bytes 12292
  209.0 77.3 %copy-start.2 = (f32[1024]{0:T(1024)S(1)}, f32[1024]{0:T(1024)}, u32[]{:S(2)}) copy-start(f32[1024]{0:T(1024)} %subtract_bitcast_fusion) | copy-start | bytes 12292
  209.0 77.3 %copy-start.6 = (f32[4]{0:T(128)S(1)}, f32[4]{0:T(128)}, u32[]{:S(2)}) copy-start(f32[4]{0:T(128)} %param.13) | copy-start | bytes 52
  209.0 77.3 %copy-start.7 = (f32[4]{0:T(128)S(1)}, f32[4]{0:T(128)}, u32[]{:S(2)}) copy-start(f32[4]{0:T(128)} %mul.43) | copy-start | bytes 52
  325.8 0.6 copy-start
Sparse Core Ops, SparseCore 0:
  9.6 84.7 all-gather.1
  100.0 102.0 all-reduce.1
where the time goes:
time: 334 us; the launch traced here: 333 us
  waiting for transfers between devices  187 us (56%)
  matrix products  77.2 us (23%)
  blocking collectives  39.3 us (12%)
  between operations  14.2 us (4%)
  other arithmetic  8.28 us (2%)
  local copies, waits for them, and re-layouts  6.9 us (2%)
    psum x1, waiting for transfers between devices, broadcast(): return lax.psum(block, axis)  100 us
    all_gather x1, waiting for transfers between devices, shards(): panel = lax.all_gather(pair_states, 'col', axis=1, tiled=True)  86.4 us
    dot_general x1, matrix products, shards(): jnp.einsum('pg,fgc->fpc', panel, screening, preferred_element_type=jnp.fl...  77.2 us
    psum x1, blocking collectives, shards(): flat = lax.psum(jnp.sum(factor * partial_value, axis=0), ('row', 'col'))  39.3 us
    convert_element_type x1, local copies, waits for them, and re-layouts, shards(): col_states.astype(jnp.float32)[None, :, :]  6.86 us
  transfers between devices with their start and end apart: 2, of which 2 were waited for; matrix products, arithmetic and copies ran while one was open for 1% of the time, Pallas kernels for 0%

commit v1 on v0

--- a/solution.py
+++ b/solution.py
@@ -2,11 +2,17 @@
 import jax.numpy as jnp
 from jax import lax
 from jax.sharding import PartitionSpec as P
+from jax.lax import all_gather
 
 
 def broadcast(block, axis, holder):
     block = jnp.where(lax.axis_index(axis) == holder, block, jnp.zeros_like(block))
-    return lax.psum(block, axis)
+
+    def ladders_launch(vector):
+        e_next = all_gather(vector, axis).sum(axis=0)
+        return e_next
+
+    return ladders_launch(block)
 
 
 def shards(pair_states, screening, qp_energy, band_energy, band_index, nodes, node_weights):

time: 334 us -> 399 us (1.19)
  waiting for transfers between devices: 187 us -> 241 us
  other arithmetic: 8.28 us -> 20.4 us
    all_gather x0 -> x1, waiting for transfers between devices: none -> 154 us  [ladders_launch(): e_next = all_gather(vector, axis).sum(axis=0)]
    psum x1 -> x0, waiting for transfers between devices: 100 us -> none  [broadcast(): return lax.psum(block, axis)]
    reduce_sum x0 -> x1, other arithmetic: none -> 12.1 us  [ladders_launch(): e_next = all_gather(vector, axis).sum(axis=0)]
where the time goes in v1:
time: 399 us
  waiting for transfers between devices  241 us (60%)
  matrix products  77.2 us (19%)
  blocking collectives  39.3 us (10%)
  other arithmetic  20.4 us (5%)
  between operations  14.2 us (4%)
  local copies, waits for them, and re-layouts  6.9 us (2%)
    all_gather x1, waiting for transfers between devices, ladders_launch(): e_next = all_gather(vector, axis).sum(axis=0)  154 us
    all_gather x1, waiting for transfers between devices, shards(): panel = lax.all_gather(pair_states, 'col', axis=1, tiled=True)  86.4 us
    dot_general x1, matrix products, shards(): jnp.einsum('pg,fgc->fpc', panel, screening, preferred_element_type=jnp.fl...  77.2 us
    psum x1, blocking collectives, shards(): flat = lax.psum(jnp.sum(factor * partial_value, axis=0), ('row', 'col'))  39.3 us
    reduce_sum x1, other arithmetic, ladders_launch(): e_next = all_gather(vector, axis).sum(axis=0)  12.1 us
  transfers between devices with their start and end apart: 2, of which 2 were waited for; matrix products, arithmetic and copies ran while one was open for 1% of the time, Pallas kernels for 0%

profile of v1, /device:TPU:0, one launch (start us, length us, event | category | flops | bytes accessed | tf_op | source)
XLA Modules:
  0.0 399.0 jit_solution(7528455744867752103)
XLA Ops:
  7.2 0.0 copy-start.8
  7.2 0.0 copy-start.3
  7.2 0.0 copy-start.5
  7.2 0.0 copy-start.4
  7.2 0.0 all-gather.4.cloned.1.call-start
  7.2 0.7 all-gather.4.cloned.1.call-update
  7.9 0.0 all-gather.6.cloned.1.call-start
  8.0 86.4 %all-gather.4.cloned.1.call-done = bf16[1024,4096]{1,0:T(8,128)(2,1)} async-done(((bf16[1024,512]{1,0:T(8,128)(2,1)}), bf16[1024,4096]{1,0:T(8,128)(2,1)}) %all-gather.4.cloned.1.call-update) | async-done | bytes 8388624 | tf_op jit(solution)/shard_map/all_gather | solution.py:20
  94.4 5.5 %dynamic-slice_select_fusion = bf16[1024,2048]{1,0:T(8,128)(2,1)} fusion(bf16[1024,4096]{1,0:T(8,128)(2,1)} %all-gather.4.cloned.1.call-done, s32[]{:T(128)S(6)} %select_n.30, pred[]{:T(512)S(6)} %eq.15), kind=kLoop, calls=%fused_computation.3 | loop fusion | flops 2097152 | bytes 8388613 | tf_op jit(solution)/shard_map/jit(_where)/select_n | solution.py:9
  99.9 0.0 all-gather.6.cloned.1.call-update
  99.9 0.0 copy-done.8
  99.9 0.5 mul.43
  100.4 0.0 copy-done.3
  100.4 0.0 copy-done.5
  100.4 0.2 select_reduce_fusion
  100.7 0.0 copy-done.4
  100.7 0.7 fusion.2
  101.4 0.7 subtract_bitcast_fusion
  102.0 153.8 %all-gather.6.cloned.1.call-done = bf16[4096,2048]{1,0:T(8,128)(2,1)} async-done(((bf16[1024,2048]{1,0:T(8,128)(2,1)}), bf16[4096,2048]{1,0:T(8,128)(2,1)}) %all-gather.6.cloned.1.call-update) | async-done | bytes 16777232 | tf_op jit(solution)/shard_map/all_gather | solution.py:12
  255.8 12.1 %reduce_sum.49 = bf16[1024,2048]{1,0:T(8,128)(2,1)} reduce(bf16[4,1024,2048]{2,1,0:T(8,128)(2,1)} %bitcast.14, bf16[]{:T(256)} %constant.41.clone.1), dimensions={0}, to_apply=%region_1.2 | reduce | flops 6291456 | bytes 20971522 | tf_op jit(solution)/shard_map/reduce_sum | solution.py:12
  267.9 6.9 %copy.13 = f32[1024,2048]{0,1:T(8,128)} copy(bf16[1024,2048]{1,0:T(8,128)(2,1)} %reduce_sum.49) | data formatting | bytes 12582912 | tf_op jit(solution)/shard_map/convert_element_type | solution.py:27
  274.8 0.0 copy-start.1
  274.8 0.0 copy-start.2
  274.8 0.0 copy-start.6
  274.8 0.0 copy-start.7
  274.8 77.2 %fusion = f32[4,1024]{1,0:T(4,128)S(1)} fusion(bf16[4,4096,2048]{2,1,0:T(8,128)(2,1)} %param.8, f32[1024,2048]{0,1:T(8,128)} %copy.13, bf16[1024,4096]{1,0:T(8,128)(2,1)} %all-gather.4.cloned.1.call-done), kind=kOutput, calls=%fused_computation.1 | convolution fusion | flops 68736253952 | bytes 83902464 | tf_op jit(solution)/shard_map/pg,fgc->fpc/dot_general | solution.py:21
  352.1 0.0 copy-done.1
  352.1 0.0 copy-done.2
  352.1 0.0 copy-done.6
  352.1 0.0 copy-done.7
  352.1 0.1 multiply_reduce_fusion
  352.2 39.3 %psum.7 = f32[8,128]{1,0:T(8,128)S(1)} all-reduce(f32[8,128]{1,0:T(8,128)S(1)} %bitcast.15), channel_id=1, replica_groups=mesh['row'=4,'col'=8] {'row','col'}, use_global_device_ids=true, to_apply=%region_4.5 | all-reduce | flops 1024 | bytes 8192 | tf_op jit(solution)/shard_map/psum | solution.py:38
  391.5 0.0 copy-start
  391.5 0.6 reduce_sum.52
  392.1 0.0 copy-done
Async XLA Ops:
  7.2 92.8 %copy-start.8 = (f32[4]{0:T(128)S(1)}, f32[4]{0:T(128)}, u32[]{:S(2)}) copy-start(f32[4]{0:T(128)} %param.12) | copy-start | bytes 52
  7.2 93.3 %copy-start.3 = (f32[2048]{0:T(1024)S(1)}, f32[2048]{0:T(1024)}, u32[]{:S(2)}) copy-start(f32[2048]{0:T(1024)} %param.10) | copy-start | bytes 24580
  7.2 93.3 %copy-start.5 = (s32[128]{0:T(128)S(1)}, s32[128]{0:T(128)}, u32[]{:S(2)}) copy-start(s32[128]{0:T(128)} %param.11) | copy-start | bytes 1540
  7.2 93.5 %copy-start.4 = (f32[8]{0:T(128)S(1)}, f32[8]{0:T(128)}, u32[]{:S(2)}) copy-start(f32[8]{0:T(128)} %param.9) | copy-start | bytes 100
  7.2 87.2 %all-gather.4.cloned.1.call-start = ((), (), s32[]{:S(2)}) async-start(), calls=%async_computation | async-start | bytes 9437184 | tf_op jit(solution)/shard_map/all_gather | solution.py:20
  7.9 247.9 %all-gather.6.cloned.1.call-start = ((), (), s32[]{:S(2)}) async-start(), calls=%async_computation.1 | async-start | bytes 20971520 | tf_op jit(solution)/shard_map/all_gather | solution.py:12
  274.8 77.3 %copy-start.1 = (f32[1024]{0:T(1024)S(1)}, f32[1024]{0:T(1024)}, u32[]{:S(2)}) copy-start(f32[1024]{0:T(1024)} %fusion.2) | copy-start | bytes 12292
  274.8 77.3 %copy-start.2 = (f32[1024]{0:T(1024)S(1)}, f32[1024]{0:T(1024)}, u32[]{:S(2)}) copy-start(f32[1024]{0:T(1024)} %subtract_bitcast_fusion) | copy-start | bytes 12292
  274.8 77.3 %copy-start.6 = (f32[4]{0:T(128)S(1)}, f32[4]{0:T(128)}, u32[]{:S(2)}) copy-start(f32[4]{0:T(128)} %param.13) | copy-start | bytes 52
  274.8 77.3 %copy-start.7 = (f32[4]{0:T(128)S(1)}, f32[4]{0:T(128)}, u32[]{:S(2)}) copy-start(f32[4]{0:T(128)} %mul.43) | copy-start | bytes 52
  391.5 0.6 copy-start
Sparse Core Ops, SparseCore 0:
  9.6 84.7 all-gather.3
  100.0 155.7 all-gather.5
